TPU v7x, 32 devices: a whole 2x2x4 slice. The times are simulated.
32 devices in a mesh: tx: 8 (over z, y), ty: 2 (over x), mem: 2 (over core).
Axes of the slice: x: 2, y: 2, z: 4, core: 2. Of those that a mesh axis runs over, the one named last changes fastest.
Arguments:
- obs_value: float32 [262144], P(('tx', 'ty', 'mem')), may hold values from -6 to 6
- obs_frac: float32 [2, 262144], P(None, ('tx', 'ty', 'mem')), may hold values from 0 to 1
- obs_cell: int32 [262144], P(('tx', 'ty', 'mem')), may hold values from 0 to 2047
- obs_layer: int32 [262144], P(('tx', 'ty', 'mem')), may hold values from 0 to 11
- obs_tile: int32 [262144], P(('tx', 'ty', 'mem')), may hold values from 0 to 15, as said below
- obs_length: int32 [32], P(('tx', 'ty', 'mem')), may hold values from 4096 to 8192, as said below
- ensemble: bfloat16 [80, 6, 2, 128, 256], P('mem', None, None, 'tx', 'ty'), may hold values from -6 to 6
Outputs:
- alpha_grad: bfloat16 [80, 2, 128, 256], P('mem', None, 'tx', 'ty')
Inputs may be any that keep to these rules, and one draw needn't show every extreme that they name: `obs_tile`: among the 8192 entries of one device's list, padding included, at most 1536 name one tile; one tile is named by exactly 1536 live entries of every device's list. `obs_length`: every fourth list is full.
All inputs are finite; a program needn't handle non-finite values.
Results may differ from a plain program's by a relative error of at most 0.001.
Values sent between devices are 32-bit elements; how exact they have to be, the bound alone decides.
A program may use at most 64 MiB of HBM per device.

v0:
```python
import math

import jax
import jax.numpy as jnp
from jax import lax
from jax.sharding import PartitionSpec as P


def shifted(block, axis, distance):
    devices = range(lax.axis_size(axis))
    route = [(i - distance, i) for i in devices if i - distance in devices]
    return lax.ppermute(block, axis, route)


def extended_2(x, sides, width):
    for axis, dim in sides:
        size, length = (lax.axis_size(axis), x.shape[dim])
        up = [(i, (i + 1) % size) for i in range(size - 1)]
        down = [(j, i) for i, j in up]
        last = lax.slice_in_dim(x, length - width, length, axis=dim)
        initial = lax.slice_in_dim(x, 0, width, axis=dim)
        before = lax.ppermute(last, axis, up)
        after = lax.ppermute(initial, axis, down)
        x = jnp.concatenate([before, x, after], axis=dim)
    return x


def smooth(padded):
    along_x = 0.25 * padded[:, :, :-2, :] + 0.5 * padded[:, :, 1:-1, :] + 0.25 * padded[:, :, 2:, :]
    return 0.25 * along_x[:, :, :, :-2] + 0.5 * along_x[:, :, :, 1:-1] + 0.25 * along_x[:, :, :, 2:]


def contract_rows(left, right):
    return lax.dot_general(
        left,
        right,
        (((0,), (0,)), ((), ())),
        precision=lax.Precision.HIGHEST,
        preferred_element_type=jnp.float32,
    )


def body(obs_value, obs_frac, obs_cell, obs_layer, obs_tile, obs_length, ensemble):
    tiles_x = lax.axis_size("tx")
    tiles_y = lax.axis_size("ty")
    tile_count = tiles_x * tiles_y
    row_count = obs_value.shape[0]
    capacity = 3 * row_count // tile_count
    slot_count = ensemble.shape[1]
    level_count = ensemble.shape[2]
    cells_x = ensemble.shape[3]
    cells_y = ensemble.shape[4]
    layer_count = slot_count * level_count
    live_rows = jnp.arange(row_count, dtype=jnp.int32) < obs_length[0]
    one_hot = (
        (obs_tile[:, None] == jnp.arange(tile_count, dtype=jnp.int32)[None, :]) & live_rows[:, None]
    ).astype(jnp.float32)
    blocks = one_hot.reshape(row_count // 128, 128, tile_count)
    lower = jnp.arange(128, dtype=jnp.int32)
    triangle = (lower[:, None] >= lower[None, :]).astype(jnp.float32)
    within = jnp.einsum("ij,bjt->bit", triangle, blocks)
    block_totals = jnp.sum(blocks, axis=1)
    offsets = jnp.cumsum(block_totals, axis=0) - block_totals
    ranking = (
        jnp.sum((within + offsets[:, None, :]) * blocks, axis=-1)
        .reshape(row_count)
        .astype(jnp.int32)
        - 1
    )
    position = obs_layer * (cells_x * cells_y) + obs_cell
    payload = jnp.stack([obs_value, obs_frac[0], obs_frac[1], position.astype(jnp.float32)], axis=1)
    send_block = math.gcd(row_count, 2048)
    slot_ids = jnp.arange(capacity, dtype=jnp.int32)

    def place_rows(step, packed):
        start = step * send_block
        hot = lax.dynamic_slice_in_dim(one_hot, start, send_block, 0)
        load = lax.dynamic_slice_in_dim(payload, start, send_block, 0)
        rank = lax.dynamic_slice_in_dim(ranking, start, send_block, 0)
        slots = (rank[:, None] == slot_ids[None, :]).astype(jnp.float32)
        left = (load[:, :, None] * hot[:, None, :]).reshape(send_block, 4 * tile_count)
        return packed + contract_rows(left, slots)

    packed = lax.fori_loop(
        0, row_count // send_block, place_rows, jnp.zeros((4 * tile_count, capacity), jnp.float32)
    )
    packed = packed.reshape(4, tile_count, capacity)
    send_floats = packed[:3]
    send_index = packed[3:4].astype(jnp.int32)
    got_floats, got_index = (
        lax.all_to_all(send_floats, ("tx", "ty"), split_axis=1, concat_axis=1, tiled=True),
        lax.all_to_all(send_index, ("tx", "ty"), split_axis=1, concat_axis=1, tiled=True),
    )
    got_count = tile_count * capacity
    values = got_floats[0].reshape(-1)
    frac_x = got_floats[1].reshape(-1)
    frac_y = got_floats[2].reshape(-1)
    spot = got_index[0].reshape(-1)
    layer = spot // (cells_x * cells_y)
    column = spot % (cells_x * cells_y)
    column_x = column // cells_y
    column_y = column % cells_y
    recv_block = math.gcd(got_count, 2048)
    layer_ids = jnp.arange(layer_count, dtype=jnp.int32)
    xs_ids = jnp.arange(cells_x + 1, dtype=jnp.int32)
    ys_ids = jnp.arange(cells_y, dtype=jnp.int32)

    def spread_rows(step, carry):
        main, rim = carry
        start = step * recv_block
        val = lax.dynamic_slice_in_dim(values, start, recv_block, 0)
        wfx = lax.dynamic_slice_in_dim(frac_x, start, recv_block, 0)
        wfy = lax.dynamic_slice_in_dim(frac_y, start, recv_block, 0)
        lay = lax.dynamic_slice_in_dim(layer, start, recv_block, 0)
        colx = lax.dynamic_slice_in_dim(column_x, start, recv_block, 0)
        coly = lax.dynamic_slice_in_dim(column_y, start, recv_block, 0)
        layer_hot = jnp.where(lay[:, None] == layer_ids[None, :], val[:, None], jnp.float32(0.0))
        weight_x = jnp.where(colx[:, None] == xs_ids[None, :], 1.0 - wfx[:, None], jnp.float32(0.0))
        weight_x = weight_x + jnp.where(
            colx[:, None] + 1 == xs_ids[None, :], wfx[:, None], jnp.float32(0.0)
        )
        weight_y = jnp.where(coly[:, None] == ys_ids[None, :], 1.0 - wfy[:, None], jnp.float32(0.0))
        weight_y = weight_y + jnp.where(
            coly[:, None] + 1 == ys_ids[None, :], wfy[:, None], jnp.float32(0.0)
        )
        rim_weight = jnp.where(coly + 1 == cells_y, wfy, jnp.float32(0.0))
        left = (layer_hot[:, :, None] * weight_x[:, None, :]).reshape(
            recv_block, layer_count * (cells_x + 1)
        )
        main = main + contract_rows(left, weight_y)
        rim = rim + contract_rows(left, rim_weight)
        return (main, rim)

    start_main = jnp.zeros((layer_count * (cells_x + 1), cells_y), jnp.float32)
    start_rim = jnp.zeros((layer_count * (cells_x + 1),), jnp.float32)
    main, rim = lax.fori_loop(0, got_count // recv_block, spread_rows, (start_main, start_rim))
    extended = main.reshape(layer_count, cells_x + 1, cells_y)
    interior = extended[:, :cells_x, :]
    east_rim = extended[:, cells_x, :]
    north_rim = rim.reshape(layer_count, cells_x + 1)
    from_south = shifted(north_rim, "ty", 1)
    interior = interior.at[:, :, 0].add(from_south[:, :cells_x])
    east_rim = east_rim.at[:, 0].add(from_south[:, cells_x])
    from_west = shifted(east_rim, "tx", 1)
    interior = interior.at[:, 0, :].add(from_west)
    grad = lax.psum(interior, "mem")
    grad_slots = grad.reshape(slot_count, level_count, cells_x, cells_y)
    contrib = jnp.sum(ensemble * grad_slots[None], axis=1)
    padded = extended_2(contrib, (("tx", 2), ("ty", 3)), 1)
    return smooth(padded).astype(jnp.bfloat16)


def solution(mesh):
    placed = (
        P(("tx", "ty", "mem")),
        P(None, ("tx", "ty", "mem")),
        P(("tx", "ty", "mem")),
        P(("tx", "ty", "mem")),
        P(("tx", "ty", "mem")),
        P(("tx", "ty", "mem")),
        P("mem", None, None, "tx", "ty"),
    )
    return jax.shard_map(
        body, mesh=mesh, in_specs=placed, out_specs=P("mem", None, "tx", "ty"), check_vma=False
    )
```

profile of v0, /device:TPU:0, one launch (start us, length us, event | category | flops | bytes accessed | tf_op | source)
XLA Modules:
  0.0 210.7 jit_solution(81586102817702164)
XLA Ops:
  11.5 20.3 %while.34 = (s32[]{:T(128)}, f32[64,1536]{1,0:T(8,128)S(1)}, f32[8192,4]{0,1:T(4,128)S(1)}, f32[8192,16]{0,1:T(8,128)S(1)}, s32[8192]{0:T(1024)S(1)}, /*index=5*/s32[]{:T(128)}, s32[]{:T(128)}, s32[]{:T(128)}, s32[]{:T(128)}) while((s32[]{:T(128)}, f32[64,1536]{1,0:T(8,128)S(1)}, f32[8192,4]{0,1:T(4,128)S(1)}, ...), condition=%wide.region_4.5_spmd.clone, body=%wide.region_3.4_spmd.clone.sunk | while | flops 2419392512 | bytes 2351265 | solution.py:84
  11.7 4.9 %fusion.59 = f32[64,1536]{1,0:T(8,128)S(1)} fusion(f32[2048,64]{0,1:T(8,128)S(1)} %bitcast.59, s32[2048]{0:T(1024)S(1)} %dynamic_slice.94, f32[64,1536]{1,0:T(8,128)S(1)} %get-tuple-element.605, pred[]{:T(512)S(6)} %compare.33), kind=kOutput, calls=%fused_computation.7.clone.1 | convolution fusion | flops 2419261440 | bytes 1318913 | tf_op jit(solution)/shard_map/while/body/eval_jaxpr/dot_general | solution.py:34
  16.7 4.9 %fusion.59 = f32[64,1536]{1,0:T(8,128)S(1)} fusion(f32[2048,64]{0,1:T(8,128)S(1)} %bitcast.59, s32[2048]{0:T(1024)S(1)} %dynamic_slice.94, f32[64,1536]{1,0:T(8,128)S(1)} %get-tuple-element.605, pred[]{:T(512)S(6)} %compare.33), kind=kOutput, calls=%fused_computation.7.clone.1 | convolution fusion | flops 2419261440 | bytes 1318913 | tf_op jit(solution)/shard_map/while/body/eval_jaxpr/dot_general | solution.py:34
  21.8 4.9 %fusion.59 = f32[64,1536]{1,0:T(8,128)S(1)} fusion(f32[2048,64]{0,1:T(8,128)S(1)} %bitcast.59, s32[2048]{0:T(1024)S(1)} %dynamic_slice.94, f32[64,1536]{1,0:T(8,128)S(1)} %get-tuple-element.605, pred[]{:T(512)S(6)} %compare.33), kind=kOutput, calls=%fused_computation.7.clone.1 | convolution fusion | flops 2419261440 | bytes 1318913 | tf_op jit(solution)/shard_map/while/body/eval_jaxpr/dot_general | solution.py:34
  26.9 4.9 %fusion.59 = f32[64,1536]{1,0:T(8,128)S(1)} fusion(f32[2048,64]{0,1:T(8,128)S(1)} %bitcast.59, s32[2048]{0:T(1024)S(1)} %dynamic_slice.94, f32[64,1536]{1,0:T(8,128)S(1)} %get-tuple-element.605, pred[]{:T(512)S(6)} %compare.33), kind=kOutput, calls=%fused_computation.7.clone.1 | convolution fusion | flops 2419261440 | bytes 1318913 | tf_op jit(solution)/shard_map/while/body/eval_jaxpr/dot_general | solution.py:34
  32.6 8.3 %all-to-all-start = ((s32[1,16,1536]{2,0,1:T(1,128)}), s32[1,16,1536]{2,0,1:T(1,128)S(1)}, u32[]{:S(2)}, u32[]{:S(2)}) async-start(s32[1,16,1536]{2,0,1:T(1,128)} %convert_element_type.35), calls=%async_computation | async-start | bytes 196608 | tf_op jit(solution)/shard_map/all_to_all | solution.py:92
  41.9 6.7 %all-to-all-done = s32[1,16,1536]{2,0,1:T(1,128)S(1)} async-done(((s32[1,16,1536]{2,0,1:T(1,128)}), s32[1,16,1536]{2,0,1:T(1,128)S(1)}, u32[]{:S(2)}, u32[]{:S(2)}) %all-to-all-start) | async-done | bytes 98336 | tf_op jit(solution)/shard_map/all_to_all | solution.py:92
  48.6 3.6 %all-to-all-start.1 = ((f32[3,16,1536]{2,0,1:T(4,128)}), f32[3,16,1536]{2,0,1:T(4,128)S(1)}, u32[]{:S(2)}, u32[]{:S(2)}) async-start(f32[3,16,1536]{2,0,1:T(4,128)} %copy.54), calls=%async_computation.1 | async-start | bytes 786432 | tf_op jit(solution)/shard_map/all_to_all | solution.py:91
  52.4 11.2 %all-to-all-done.1 = f32[3,16,1536]{2,0,1:T(4,128)S(1)} async-done(((f32[3,16,1536]{2,0,1:T(4,128)}), f32[3,16,1536]{2,0,1:T(4,128)S(1)}, u32[]{:S(2)}, u32[]{:S(2)}) %all-to-all-start.1) | async-done | bytes 294944 | tf_op jit(solution)/shard_map/all_to_all | solution.py:91
  63.7 87.0 %while.35 = (s32[]{:T(128)}, f32[204,128]{1,0:T(8,128)S(1)}, f32[204]{0:T(256)S(1)}, s32[24576]{0:T(1024)S(1)}, f32[24576]{0:T(1024)S(1)}, /*index=5*/s32[24576]...) while((s32[]{:T(128)}, f32[204,128]{1,0:T(8,128)S(1)}, ...), condition=%wide.region_6.7_spmd.clone.clone, body=%wide.region_5.6_spmd.clone.clone.sunk | while | flops 648760704 | bytes 15973794 | solution.py:136
  64.2 1.4 mul.212
  65.6 3.9 %convolution_add_fusion.3 = f32[204,128]{1,0:T(8,128)S(1)} fusion(f32[2048,204]{0,1:T(8,128)} %mul.212, f32[2048]{0:T(1024)S(1)} %get-tuple-element.592, s32[2048]{0:T(1024)S(1)} %broadcast_add_fusion.5, f32[2048]{0:T(1024)S(1)} %broadcast_subtract_fusion.3, s32[2048]{0:T(1024)S(1)} %get-tuple-element.593, f32[204,128]{1,0:T(8,128)S(1)} %get-tuple-element.636, ...), kind=kOutput, calls=%fused_computation.14.clone.1 | convolution fusion | flops 643091456 | bytes 1912833 | tf_op jit(solution)/shard_map/while/body/eval_jaxpr/dot_general | solution.py:34
  69.5 1.4 fusion.65
  71.4 1.4 mul.212
  72.9 3.9 %convolution_add_fusion.3 = f32[204,128]{1,0:T(8,128)S(1)} fusion(f32[2048,204]{0,1:T(8,128)} %mul.212, f32[2048]{0:T(1024)S(1)} %get-tuple-element.592, s32[2048]{0:T(1024)S(1)} %broadcast_add_fusion.5, f32[2048]{0:T(1024)S(1)} %broadcast_subtract_fusion.3, s32[2048]{0:T(1024)S(1)} %get-tuple-element.593, f32[204,128]{1,0:T(8,128)S(1)} %get-tuple-element.636, ...), kind=kOutput, calls=%fused_computation.14.clone.1 | convolution fusion | flops 643091456 | bytes 1912833 | tf_op jit(solution)/shard_map/while/body/eval_jaxpr/dot_general | solution.py:34
  76.8 1.4 fusion.65
  78.7 1.4 mul.212
  80.1 3.9 %convolution_add_fusion.3 = f32[204,128]{1,0:T(8,128)S(1)} fusion(f32[2048,204]{0,1:T(8,128)} %mul.212, f32[2048]{0:T(1024)S(1)} %get-tuple-element.592, s32[2048]{0:T(1024)S(1)} %broadcast_add_fusion.5, f32[2048]{0:T(1024)S(1)} %broadcast_subtract_fusion.3, s32[2048]{0:T(1024)S(1)} %get-tuple-element.593, f32[204,128]{1,0:T(8,128)S(1)} %get-tuple-element.636, ...), kind=kOutput, calls=%fused_computation.14.clone.1 | convolution fusion | flops 643091456 | bytes 1912833 | tf_op jit(solution)/shard_map/while/body/eval_jaxpr/dot_general | solution.py:34
  84.0 1.4 fusion.65
  85.9 1.4 mul.212
  87.4 3.9 %convolution_add_fusion.3 = f32[204,128]{1,0:T(8,128)S(1)} fusion(f32[2048,204]{0,1:T(8,128)} %mul.212, f32[2048]{0:T(1024)S(1)} %get-tuple-element.592, s32[2048]{0:T(1024)S(1)} %broadcast_add_fusion.5, f32[2048]{0:T(1024)S(1)} %broadcast_subtract_fusion.3, s32[2048]{0:T(1024)S(1)} %get-tuple-element.593, f32[204,128]{1,0:T(8,128)S(1)} %get-tuple-element.636, ...), kind=kOutput, calls=%fused_computation.14.clone.1 | convolution fusion | flops 643091456 | bytes 1912833 | tf_op jit(solution)/shard_map/while/body/eval_jaxpr/dot_general | solution.py:34
  91.3 1.4 fusion.65
  93.2 1.4 mul.212
  94.6 3.9 %convolution_add_fusion.3 = f32[204,128]{1,0:T(8,128)S(1)} fusion(f32[2048,204]{0,1:T(8,128)} %mul.212, f32[2048]{0:T(1024)S(1)} %get-tuple-element.592, s32[2048]{0:T(1024)S(1)} %broadcast_add_fusion.5, f32[2048]{0:T(1024)S(1)} %broadcast_subtract_fusion.3, s32[2048]{0:T(1024)S(1)} %get-tuple-element.593, f32[204,128]{1,0:T(8,128)S(1)} %get-tuple-element.636, ...), kind=kOutput, calls=%fused_computation.14.clone.1 | convolution fusion | flops 643091456 | bytes 1912833 | tf_op jit(solution)/shard_map/while/body/eval_jaxpr/dot_general | solution.py:34
  98.5 1.4 fusion.65
  100.4 1.4 mul.212
  101.9 3.9 %convolution_add_fusion.3 = f32[204,128]{1,0:T(8,128)S(1)} fusion(f32[2048,204]{0,1:T(8,128)} %mul.212, f32[2048]{0:T(1024)S(1)} %get-tuple-element.592, s32[2048]{0:T(1024)S(1)} %broadcast_add_fusion.5, f32[2048]{0:T(1024)S(1)} %broadcast_subtract_fusion.3, s32[2048]{0:T(1024)S(1)} %get-tuple-element.593, f32[204,128]{1,0:T(8,128)S(1)} %get-tuple-element.636, ...), kind=kOutput, calls=%fused_computation.14.clone.1 | convolution fusion | flops 643091456 | bytes 1912833 | tf_op jit(solution)/shard_map/while/body/eval_jaxpr/dot_general | solution.py:34
  105.8 1.4 fusion.65
  107.7 1.4 mul.212
  109.1 3.9 %convolution_add_fusion.3 = f32[204,128]{1,0:T(8,128)S(1)} fusion(f32[2048,204]{0,1:T(8,128)} %mul.212, f32[2048]{0:T(1024)S(1)} %get-tuple-element.592, s32[2048]{0:T(1024)S(1)} %broadcast_add_fusion.5, f32[2048]{0:T(1024)S(1)} %broadcast_subtract_fusion.3, s32[2048]{0:T(1024)S(1)} %get-tuple-element.593, f32[204,128]{1,0:T(8,128)S(1)} %get-tuple-element.636, ...), kind=kOutput, calls=%fused_computation.14.clone.1 | convolution fusion | flops 643091456 | bytes 1912833 | tf_op jit(solution)/shard_map/while/body/eval_jaxpr/dot_general | solution.py:34
  113.0 1.4 fusion.65
  114.9 1.4 mul.212
  116.4 3.9 %convolution_add_fusion.3 = f32[204,128]{1,0:T(8,128)S(1)} fusion(f32[2048,204]{0,1:T(8,128)} %mul.212, f32[2048]{0:T(1024)S(1)} %get-tuple-element.592, s32[2048]{0:T(1024)S(1)} %broadcast_add_fusion.5, f32[2048]{0:T(1024)S(1)} %broadcast_subtract_fusion.3, s32[2048]{0:T(1024)S(1)} %get-tuple-element.593, f32[204,128]{1,0:T(8,128)S(1)} %get-tuple-element.636, ...), kind=kOutput, calls=%fused_computation.14.clone.1 | convolution fusion | flops 643091456 | bytes 1912833 | tf_op jit(solution)/shard_map/while/body/eval_jaxpr/dot_general | solution.py:34
  122.2 1.4 mul.212
  123.6 3.9 %convolution_add_fusion.3 = f32[204,128]{1,0:T(8,128)S(1)} fusion(f32[2048,204]{0,1:T(8,128)} %mul.212, f32[2048]{0:T(1024)S(1)} %get-tuple-element.592, s32[2048]{0:T(1024)S(1)} %broadcast_add_fusion.5, f32[2048]{0:T(1024)S(1)} %broadcast_subtract_fusion.3, s32[2048]{0:T(1024)S(1)} %get-tuple-element.593, f32[204,128]{1,0:T(8,128)S(1)} %get-tuple-element.636, ...), kind=kOutput, calls=%fused_computation.14.clone.1 | convolution fusion | flops 643091456 | bytes 1912833 | tf_op jit(solution)/shard_map/while/body/eval_jaxpr/dot_general | solution.py:34
  129.4 1.4 mul.212
  130.9 3.9 %convolution_add_fusion.3 = f32[204,128]{1,0:T(8,128)S(1)} fusion(f32[2048,204]{0,1:T(8,128)} %mul.212, f32[2048]{0:T(1024)S(1)} %get-tuple-element.592, s32[2048]{0:T(1024)S(1)} %broadcast_add_fusion.5, f32[2048]{0:T(1024)S(1)} %broadcast_subtract_fusion.3, s32[2048]{0:T(1024)S(1)} %get-tuple-element.593, f32[204,128]{1,0:T(8,128)S(1)} %get-tuple-element.636, ...), kind=kOutput, calls=%fused_computation.14.clone.1 | convolution fusion | flops 643091456 | bytes 1912833 | tf_op jit(solution)/shard_map/while/body/eval_jaxpr/dot_general | solution.py:34
  136.7 1.4 mul.212
  138.1 3.9 %convolution_add_fusion.3 = f32[204,128]{1,0:T(8,128)S(1)} fusion(f32[2048,204]{0,1:T(8,128)} %mul.212, f32[2048]{0:T(1024)S(1)} %get-tuple-element.592, s32[2048]{0:T(1024)S(1)} %broadcast_add_fusion.5, f32[2048]{0:T(1024)S(1)} %broadcast_subtract_fusion.3, s32[2048]{0:T(1024)S(1)} %get-tuple-element.593, f32[204,128]{1,0:T(8,128)S(1)} %get-tuple-element.636, ...), kind=kOutput, calls=%fused_computation.14.clone.1 | convolution fusion | flops 643091456 | bytes 1912833 | tf_op jit(solution)/shard_map/while/body/eval_jaxpr/dot_general | solution.py:34
  143.9 1.4 mul.212
  145.4 3.9 %convolution_add_fusion.3 = f32[204,128]{1,0:T(8,128)S(1)} fusion(f32[2048,204]{0,1:T(8,128)} %mul.212, f32[2048]{0:T(1024)S(1)} %get-tuple-element.592, s32[2048]{0:T(1024)S(1)} %broadcast_add_fusion.5, f32[2048]{0:T(1024)S(1)} %broadcast_subtract_fusion.3, s32[2048]{0:T(1024)S(1)} %get-tuple-element.593, f32[204,128]{1,0:T(8,128)S(1)} %get-tuple-element.636, ...), kind=kOutput, calls=%fused_computation.14.clone.1 | convolution fusion | flops 643091456 | bytes 1912833 | tf_op jit(solution)/shard_map/while/body/eval_jaxpr/dot_general | solution.py:34
  150.8 2.6 %collective-permute-start = (f32[12,17]{1,0:T(8,128)S(1)}, f32[12,17]{1,0:T(8,128)S(1)}, u32[]{:S(2)}, u32[]{:S(2)}) collective-permute-start(f32[12,17]{1,0:T(8,128)S(1)} %reshape.290), channel_id=1, source_target_pairs={{0,2},{1,3},{4,6},{5,7},{8,10},{9,11},{12,14},{13,15},{16,18},{17,... | collective-permute-start | bytes 2456 | tf_op jit(solution)/shard_map/ppermute | solution.py:12
  155.5 2.8 %collective-permute-start.1 = (f32[12,128]{1,0:T(8,128)S(1)}, f32[12,128]{1,0:T(8,128)S(1)}, u32[]{:S(2)}, u32[]{:S(2)}) collective-permute-start(f32[12,128]{1,0:T(8,128)S(1)} %scatter-add.11), channel_id=1, source_target_pairs={{0,4},{4,8},{8,12},{12,16},{16,20},{20,24},{24,28},{1,5},{5,9},{9,... | collective-permute-start | bytes 18440 | tf_op jit(solution)/shard_map/ppermute | solution.py:12
  160.4 19.5 %all-reduce.2.cloned.1.call-done = f32[6,2,16,128]{3,2,1,0:T(8,128)} async-done(((f32[6,2,16,128]{3,2,1,0:T(8,128)}), f32[6,2,16,128]{3,2,1,0:T(8,128)}) %all-reduce.2.cloned.1.call-update) | async-done | bytes 98320 | tf_op jit(solution)/shard_map/psum | solution.py:146
  181.3 3.7 %collective-permute-start.2 = (f32[40,2,1,128]{3,0,2,1:T(8,128)S(1)}, f32[40,2,1,128]{3,0,2,1:T(8,128)S(1)}, u32[]{:S(2)}, u32[]{:S(2)}) collective-permute-start(f32[40,2,1,128]{3,0,2,1:T(8,128)S(1)} %copy.61), channel_id=1, source_target_pairs={{0,4},{4,8},{8,12},{12,16},{16,20},{20,24},{24,28},{1,5},{5,9},{9,... | collective-permute-start | bytes 122888 | tf_op jit(solution)/shard_map/ppermute | solution.py:22
  186.7 4.2 %collective-permute-done.3 = f32[40,2,1,128]{3,0,2,1:T(8,128)S(1)} collective-permute-done((f32[40,2,1,128]{3,0,2,1:T(8,128)S(1)}, f32[40,2,1,128]{3,0,2,1:T(8,128)S(1)}, u32[]{:S(2)}, u32[]{:S(2)}) %collective-permute-start.3) | collective-permute-done | bytes 40992 | tf_op jit(solution)/shard_map/ppermute | solution.py:23
  191.9 3.4 %collective-permute-start.4 = (f32[40,2,18,1]{0,2,3,1:T(8,128)S(1)}, f32[40,2,18,1]{0,2,3,1:T(8,128)S(1)}, u32[]{:S(2)}, u32[]{:S(2)}) collective-permute-start(f32[40,2,18,1]{0,2,3,1:T(8,128)S(1)} %copy.65), channel_id=1, source_target_pairs={{0,2},{1,3},{4,6},{5,7},{8,10},{9,11},{12,14},{13,15},{16,18},{17,... | collective-permute-start | bytes 17288 | tf_op jit(solution)/shard_map/ppermute | solution.py:22
  197.7 3.8 %collective-permute-done.5 = f32[40,2,18,1]{0,2,3,1:T(8,128)S(1)} collective-permute-done((f32[40,2,18,1]{0,2,3,1:T(8,128)S(1)}, f32[40,2,18,1]{0,2,3,1:T(8,128)S(1)}, u32[]{:S(2)}, u32[]{:S(2)}) %collective-permute-start.5) | collective-permute-done | bytes 5792 | tf_op jit(solution)/shard_map/ppermute | solution.py:23
  (235 shorter events, 31.4 us)
Async XLA Ops:
  6.5 4.8 %copy-start.2 = (s32[8192]{0:T(1024)S(1)}, s32[8192]{0:T(1024)}, u32[]{:S(2)}) copy-start(s32[8192]{0:T(1024)} %param.19) | copy-start | bytes 98308
  6.5 4.8 %copy-start.3 = (s32[8192]{0:T(1024)S(1)}, s32[8192]{0:T(1024)}, u32[]{:S(2)}) copy-start(s32[8192]{0:T(1024)} %param.20) | copy-start | bytes 98308
  6.5 4.8 %copy-start.4 = (f32[8192]{0:T(1024)S(1)}, f32[8192]{0:T(1024)}, u32[]{:S(2)}) copy-start(f32[8192]{0:T(1024)} %param.17) | copy-start | bytes 98308
  32.6 16.0 %all-to-all-start = ((s32[1,16,1536]{2,0,1:T(1,128)}), s32[1,16,1536]{2,0,1:T(1,128)S(1)}, u32[]{:S(2)}, u32[]{:S(2)}) async-start(s32[1,16,1536]{2,0,1:T(1,128)} %convert_element_type.35), calls=%async_computation | async-start | bytes 196608 | tf_op jit(solution)/shard_map/all_to_all | solution.py:92
  48.6 14.9 %all-to-all-start.1 = ((f32[3,16,1536]{2,0,1:T(4,128)}), f32[3,16,1536]{2,0,1:T(4,128)S(1)}, u32[]{:S(2)}, u32[]{:S(2)}) async-start(f32[3,16,1536]{2,0,1:T(4,128)} %copy.54), calls=%async_computation.1 | async-start | bytes 786432 | tf_op jit(solution)/shard_map/all_to_all | solution.py:91
  52.1 127.7 %all-reduce.2.cloned.1.call-start = ((), (), s32[]{:S(2)}) async-start(), calls=%async_computation.2 | async-start | bytes 196608 | tf_op jit(solution)/shard_map/psum | solution.py:146
  65.6 3.9 %copy-start = (f32[2048,204]{0,1:T(8,128)S(1)}, f32[2048,204]{0,1:T(8,128)}, u32[]{:S(2)}) copy-start(f32[2048,204]{0,1:T(8,128)} %mul.212) | copy-start | bytes 5013508 | tf_op jit(solution)/shard_map/while
  72.8 3.9 %copy-start = (f32[2048,204]{0,1:T(8,128)S(1)}, f32[2048,204]{0,1:T(8,128)}, u32[]{:S(2)}) copy-start(f32[2048,204]{0,1:T(8,128)} %mul.212) | copy-start | bytes 5013508 | tf_op jit(solution)/shard_map/while
  80.1 3.9 %copy-start = (f32[2048,204]{0,1:T(8,128)S(1)}, f32[2048,204]{0,1:T(8,128)}, u32[]{:S(2)}) copy-start(f32[2048,204]{0,1:T(8,128)} %mul.212) | copy-start | bytes 5013508 | tf_op jit(solution)/shard_map/while
  87.3 3.9 %copy-start = (f32[2048,204]{0,1:T(8,128)S(1)}, f32[2048,204]{0,1:T(8,128)}, u32[]{:S(2)}) copy-start(f32[2048,204]{0,1:T(8,128)} %mul.212) | copy-start | bytes 5013508 | tf_op jit(solution)/shard_map/while
  94.6 3.9 %copy-start = (f32[2048,204]{0,1:T(8,128)S(1)}, f32[2048,204]{0,1:T(8,128)}, u32[]{:S(2)}) copy-start(f32[2048,204]{0,1:T(8,128)} %mul.212) | copy-start | bytes 5013508 | tf_op jit(solution)/shard_map/while
  101.8 3.9 %copy-start = (f32[2048,204]{0,1:T(8,128)S(1)}, f32[2048,204]{0,1:T(8,128)}, u32[]{:S(2)}) copy-start(f32[2048,204]{0,1:T(8,128)} %mul.212) | copy-start | bytes 5013508 | tf_op jit(solution)/shard_map/while
  109.1 3.9 %copy-start = (f32[2048,204]{0,1:T(8,128)S(1)}, f32[2048,204]{0,1:T(8,128)}, u32[]{:S(2)}) copy-start(f32[2048,204]{0,1:T(8,128)} %mul.212) | copy-start | bytes 5013508 | tf_op jit(solution)/shard_map/while
  116.3 3.9 %copy-start = (f32[2048,204]{0,1:T(8,128)S(1)}, f32[2048,204]{0,1:T(8,128)}, u32[]{:S(2)}) copy-start(f32[2048,204]{0,1:T(8,128)} %mul.212) | copy-start | bytes 5013508 | tf_op jit(solution)/shard_map/while
  123.6 3.9 %copy-start = (f32[2048,204]{0,1:T(8,128)S(1)}, f32[2048,204]{0,1:T(8,128)}, u32[]{:S(2)}) copy-start(f32[2048,204]{0,1:T(8,128)} %mul.212) | copy-start | bytes 5013508 | tf_op jit(solution)/shard_map/while
  130.9 3.9 %copy-start = (f32[2048,204]{0,1:T(8,128)S(1)}, f32[2048,204]{0,1:T(8,128)}, u32[]{:S(2)}) copy-start(f32[2048,204]{0,1:T(8,128)} %mul.212) | copy-start | bytes 5013508 | tf_op jit(solution)/shard_map/while
  138.1 3.9 %copy-start = (f32[2048,204]{0,1:T(8,128)S(1)}, f32[2048,204]{0,1:T(8,128)}, u32[]{:S(2)}) copy-start(f32[2048,204]{0,1:T(8,128)} %mul.212) | copy-start | bytes 5013508 | tf_op jit(solution)/shard_map/while
  145.4 3.9 %copy-start = (f32[2048,204]{0,1:T(8,128)S(1)}, f32[2048,204]{0,1:T(8,128)}, u32[]{:S(2)}) copy-start(f32[2048,204]{0,1:T(8,128)} %mul.212) | copy-start | bytes 5013508 | tf_op jit(solution)/shard_map/while
  150.7 29.1 %copy-start.1 = (bf16[40,6,2,16,128]{4,3,2,1,0:T(8,128)(2,1)S(1)}, bf16[40,6,2,16,128]{4,3,2,1,0:T(8,128)(2,1)}, u32[]{:S(2)}) copy-start(bf16[40,6,2,16,128]{4,3,2,1,0:T(8,128)(2,1)} %param.23) | copy-start | bytes 5898244
  150.8 3.9 %collective-permute-start = (f32[12,17]{1,0:T(8,128)S(1)}, f32[12,17]{1,0:T(8,128)S(1)}, u32[]{:S(2)}, u32[]{:S(2)}) collective-permute-start(f32[12,17]{1,0:T(8,128)S(1)} %reshape.290), channel_id=1, source_target_pairs={{0,2},{1,3},{4,6},{5,7},{8,10},{9,11},{12,14},{13,15},{16,18},{17,... | collective-permute-start | bytes 2456 | tf_op jit(solution)/shard_map/ppermute | solution.py:12
  155.5 4.1 %collective-permute-start.1 = (f32[12,128]{1,0:T(8,128)S(1)}, f32[12,128]{1,0:T(8,128)S(1)}, u32[]{:S(2)}, u32[]{:S(2)}) collective-permute-start(f32[12,128]{1,0:T(8,128)S(1)} %scatter-add.11), channel_id=1, source_target_pairs={{0,4},{4,8},{8,12},{12,16},{16,20},{20,24},{24,28},{1,5},{5,9},{9,... | collective-permute-start | bytes 18440 | tf_op jit(solution)/shard_map/ppermute | solution.py:12
  181.3 5.3 %collective-permute-start.2 = (f32[40,2,1,128]{3,0,2,1:T(8,128)S(1)}, f32[40,2,1,128]{3,0,2,1:T(8,128)S(1)}, u32[]{:S(2)}, u32[]{:S(2)}) collective-permute-start(f32[40,2,1,128]{3,0,2,1:T(8,128)S(1)} %copy.61), channel_id=1, source_target_pairs={{0,4},{4,8},{8,12},{12,16},{16,20},{20,24},{24,28},{1,5},{5,9},{9,... | collective-permute-start | bytes 122888 | tf_op jit(solution)/shard_map/ppermute | solution.py:22
  185.0 5.9 %collective-permute-start.3 = (f32[40,2,1,128]{3,0,2,1:T(8,128)S(1)}, f32[40,2,1,128]{3,0,2,1:T(8,128)S(1)}, u32[]{:S(2)}, u32[]{:S(2)}) collective-permute-start(f32[40,2,1,128]{3,0,2,1:T(8,128)S(1)} %copy.62), channel_id=1, source_target_pairs={{4,0},{8,4},{12,8},{16,12},{20,16},{24,20},{28,24},{5,1},{9,5},{13... | collective-permute-start | bytes 122888 | tf_op jit(solution)/shard_map/ppermute | solution.py:23
  191.9 5.4 %collective-permute-start.4 = (f32[40,2,18,1]{0,2,3,1:T(8,128)S(1)}, f32[40,2,18,1]{0,2,3,1:T(8,128)S(1)}, u32[]{:S(2)}, u32[]{:S(2)}) collective-permute-start(f32[40,2,18,1]{0,2,3,1:T(8,128)S(1)} %copy.65), channel_id=1, source_target_pairs={{0,2},{1,3},{4,6},{5,7},{8,10},{9,11},{12,14},{13,15},{16,18},{17,... | collective-permute-start | bytes 17288 | tf_op jit(solution)/shard_map/ppermute | solution.py:22
  195.8 5.7 %collective-permute-start.5 = (f32[40,2,18,1]{0,2,3,1:T(8,128)S(1)}, f32[40,2,18,1]{0,2,3,1:T(8,128)S(1)}, u32[]{:S(2)}, u32[]{:S(2)}) collective-permute-start(f32[40,2,18,1]{0,2,3,1:T(8,128)S(1)} %copy.66), channel_id=1, source_target_pairs={{2,0},{3,1},{6,4},{7,5},{10,8},{11,9},{14,12},{15,13},{18,16},{19,... | collective-permute-start | bytes 17288 | tf_op jit(solution)/shard_map/ppermute | solution.py:23
Sparse Core Ops, SparseCore 0:
  160.5 19.3 all-reduce.1
where the time goes:
time: 211 us
  matrix products  84.9 us (40%)
  waiting for transfers between devices  47.1 us (22%)
  starting transfers between devices  26.9 us (13%)
  local copies, waits for them, and re-layouts  25 us (12%)
  between operations  14.4 us (7%)
  other arithmetic  11 us (5%)
    dot_general x28, matrix products, contract_rows(): lax.dot_general(left, right, (((0,), (0,)), ((), ())), precision=lax.Prec...  83.7 us
    psum x1, waiting for transfers between devices, body(): grad = lax.psum(interior, 'mem')  19.5 us
    mul x12, local copies, waits for them, and re-layouts, spread_rows(): layer_hot[:, :, None] * weight_x[:, None, :]  17.2 us
    all_to_all x1, waiting for transfers between devices, body(): lax.all_to_all(send_floats, ('tx', 'ty'), split_axis=1, concat_axis=1, ti...  11.2 us
    all_to_all x1, starting transfers between devices, body(): lax.all_to_all(send_index, ('tx', 'ty'), split_axis=1, concat_axis=1, til...  8.34 us
    ppermute x2, waiting for transfers between devices, extended_2(): after = lax.ppermute(initial, axis, down)  8.04 us
    ppermute x2, starting transfers between devices, extended_2(): before = lax.ppermute(last, axis, up)  7.05 us
    all_to_all x1, waiting for transfers between devices, body(): lax.all_to_all(send_index, ('tx', 'ty'), split_axis=1, concat_axis=1, til...  6.68 us
  transfers between devices with their start and end apart: 9, of which 8 were waited for; matrix products, arithmetic and copies ran while one was open for 2% of the time, Pallas kernels for 0%

commit v1 on v0

v1 whole, which is shorter than its diff:
```python
import functools

import jax
import jax.numpy as jnp
from jax import lax
from jax.experimental import pallas as pl
from jax.experimental.pallas import tpu as pltpu
from jax.sharding import PartitionSpec as P

MESH = pl.DeviceIdType.MESH
F32 = jnp.float32
BF16 = jnp.bfloat16
LO = 256


def up_to(n, m):
    return (n + m - 1) // m * m


def split(x):
    high = x.astype(BF16)
    low = (x - high.astype(F32)).astype(BF16)
    return high, low


def dot_nt(a, b, precision=None):
    return lax.dot_general(
        a, b, (((1,), (1,)), ((), ())), precision=precision, preferred_element_type=F32
    )


def flat(rows):
    return jnp.concatenate([rows[i : i + 1] for i in range(rows.shape[0])], axis=1)


def hot(ids, code, on):
    return jnp.where(ids == code, on, jnp.zeros((), on.dtype))


def pack_kernel(tiles, hi, cells, value, frac, cell, layer, tile, length, out, acc, code_s, lo_s, val_s, pos_s):
    rows = value.shape[0]
    lanes = 128
    row_id = lax.broadcasted_iota(jnp.int32, (rows, lanes), 0)
    lane_id = lax.broadcasted_iota(jnp.int32, (rows, lanes), 1)
    tile_v = tile[...]
    masks = [jnp.where(tile_v == t, 1.0, 0.0).astype(F32) for t in range(tiles)]
    stacked = jnp.concatenate(masks, axis=0).astype(BF16)
    a = lax.broadcasted_iota(jnp.int32, (lanes, 2 * lanes), 0)
    b = lax.broadcasted_iota(jnp.int32, (lanes, 2 * lanes), 1)
    upper = jnp.where((a <= b) | (b >= lanes), 1.0, 0.0).astype(BF16)
    sums = jnp.dot(stacked, upper, preferred_element_type=F32)
    totals = jnp.concatenate(
        [sums[t * rows : (t + 1) * rows, lanes:] for t in range(tiles)], axis=1
    ).astype(BF16)
    c = lax.broadcasted_iota(jnp.int32, (rows, rows), 0)
    d = lax.broadcasted_iota(jnp.int32, (rows, rows), 1)
    lower = jnp.where(d < c, 1.0, 0.0).astype(BF16)
    offsets = jnp.dot(lower, totals, preferred_element_type=F32)
    rank = jnp.full((rows, lanes), -1.0, F32)
    for t in range(tiles):
        inner = sums[t * rows : (t + 1) * rows, :lanes] + offsets[:, t * lanes : (t + 1) * lanes]
        rank = rank + masks[t] * inner
    rank = rank.astype(jnp.int32)
    code_s[...] = tile_v * hi + rank // LO
    lo_s[...] = rank % LO
    live = row_id * lanes + lane_id < length[0]
    val_s[...] = jnp.where(live, value[...], 0.0)
    pos_s[...] = layer[...] * cells + cell[...]
    acc[...] = jnp.zeros_like(acc)
    step_rows = 8
    width = step_rows * lanes
    groups = tiles * hi
    group_id = lax.broadcasted_iota(jnp.int32, (groups, width), 0)
    lo_id = lax.broadcasted_iota(jnp.int32, (LO, width), 0)
    for s in range(rows // step_rows):
        here = pl.ds(s * step_rows, step_rows)
        along = pl.ds(s * width, width)
        code = flat(code_s[here, :])
        low_hot = jnp.where(lo_id == flat(lo_s[here, :]), 1.0, 0.0).astype(BF16)
        pos = flat(pos_s[here, :])
        pos_low = pos % 128
        fields = [
            split(flat(val_s[here, :])),
            split(frac[0:1, along]),
            split(frac[1:2, along]),
            ((pos - pos_low).astype(F32).astype(BF16), pos_low.astype(F32).astype(BF16)),
        ]
        mine = group_id == code
        for part in range(2):
            left = jnp.concatenate(
                [jnp.where(mine, f[part].astype(F32), 0.0) for f in fields], axis=0
            ).astype(BF16)
            acc[...] += dot_nt(left, low_hot)
    for t in range(tiles):
        for f in range(4):
            start = f * groups + t * hi
            out[t, f * hi : (f + 1) * hi, :] = acc[start : start + hi, :]


def main_kernel(dims, packed, ens, out, recv, acc, acc_in, gt, east_in, north_in, corner_in, con, west_h, east_h,
                send_w, send_e, edge, edge_n, edge_s, ens_v,
                s_send, s_recv, p_sem, rim_send, rim_recv, halo_send, halo_recv, local_sem):
    n_tx, n_ty, n_mem, hi, layers, cx, cy, members, slots, levels = dims
    tiles = n_tx * n_ty
    tx, ty, mem = lax.axis_index("tx"), lax.axis_index("ty"), lax.axis_index("mem")
    me = tx * n_ty + ty
    load = pltpu.make_async_copy(ens, ens_v, local_sem)
    load.start()

    barrier = pltpu.get_barrier_semaphore()

    def greet(k, c):
        t = lax.rem(me + k, tiles)
        pl.semaphore_signal(barrier, inc=1, device_id=(t // n_ty, lax.rem(t, n_ty), mem), device_id_type=MESH)
        return c

    lax.fori_loop(1, tiles, greet, 0)
    partner = (tx, ty, lax.rem(mem + 1, n_mem))
    pl.semaphore_signal(barrier, inc=1, device_id=partner, device_id_type=MESH)
    pl.semaphore_wait(barrier, tiles)

    def copy_to(t):
        return pltpu.make_async_remote_copy(
            src_ref=packed.at[t], dst_ref=recv.at[me], send_sem=s_send.at[t], recv_sem=s_recv.at[me],
            device_id=(t // n_ty, lax.rem(t, n_ty), mem), device_id_type=MESH)

    def send(k, c):
        copy_to(lax.rem(me + k, tiles)).start()
        return c

    lax.fori_loop(1, tiles, send, 0)

    width = hi * LO
    r_rows = up_to(layers * cx + layers, 16)
    y_rows = up_to(cy + 1, 16)
    r_id = lax.broadcasted_iota(jnp.int32, (r_rows, width), 0)
    y_id = lax.broadcasted_iota(jnp.int32, (y_rows, width), 0)
    cells = cx * cy

    def spread(block):
        val, fx, fy, pos = [flat(block[f * hi : (f + 1) * hi]) for f in range(4)]
        pos = pos.astype(jnp.int32)
        lay = pos // cells
        col = pos % cells
        x = col // cy
        y = col % cy
        c1 = lay * cx + x
        c2 = jnp.where(x == cx - 1, layers * cx + lay, c1 + 1)
        left = jnp.where(r_id == c1, val * (1.0 - fx), jnp.where(r_id == c2, val * fx, 0.0))
        right = jnp.where(y_id == y, 1.0 - fy, jnp.where(y_id == y + 1, fy, 0.0))
        lh, ll = split(left)
        rh, rl = split(right)
        acc[0:y_rows, 0:r_rows] += dot_nt(rh, lh) + dot_nt(rl, lh) + dot_nt(rh, ll)

    acc[...] = jnp.zeros_like(acc)
    spread(packed[me])

    def receive(k, c):
        src = lax.rem(me + tiles - k, tiles)
        pltpu.make_async_remote_copy(
            src_ref=packed.at[src], dst_ref=recv.at[src], send_sem=s_send.at[src], recv_sem=s_recv.at[src],
            device_id=(tx, ty, mem), device_id_type=MESH).wait_recv()
        spread(recv[src])
        return c

    lax.fori_loop(1, tiles, receive, 0)

    def drain(k, c):
        copy_to(lax.rem(me + k, tiles)).wait_send()
        return c

    lax.fori_loop(1, tiles, drain, 0)

    swap = pltpu.make_async_remote_copy(
        src_ref=acc.at[pl.ds(0, y_rows)], dst_ref=acc_in, send_sem=p_sem.at[0], recv_sem=p_sem.at[1],
        device_id=partner, device_id_type=MESH)
    swap.start()
    swap.wait()
    acc[0:y_rows, :] += acc_in[...]
    gt[...] = acc[...].T

    east_dev = (lax.rem(tx + 1, n_tx), ty, mem)
    west_dev = (lax.rem(tx + n_tx - 1, n_tx), ty, mem)
    north_dev = (tx, lax.rem(ty + 1, n_ty), mem)
    south_dev = (tx, lax.rem(ty + n_ty - 1, n_ty), mem)
    corner_dev = (lax.rem(tx + 1, n_tx), lax.rem(ty + 1, n_ty), mem)
    rim_rows = pl.ds(layers * cx, 16)
    rims = [
        pltpu.make_async_remote_copy(
            src_ref=s, dst_ref=d, send_sem=rim_send.at[i], recv_sem=rim_recv.at[i], device_id=dev,
            device_id_type=MESH)
        for i, (s, d, dev) in enumerate([
            (gt.at[rim_rows, pl.ds(0, cy)], east_in, east_dev),
            (acc.at[pl.ds(cy, 8)], north_in, north_dev),
            (gt.at[rim_rows, pl.ds(cy, cy)], corner_in, corner_dev),
        ])
    ]
    for c in rims:
        c.start()
    for c in rims:
        c.wait()
    from_west = (tx > 0).astype(F32)
    from_south = (ty > 0).astype(F32)
    north = jnp.concatenate([north_in[...] * from_south, jnp.zeros((cy - 8, north_in.shape[1]), F32)], axis=0)
    grad = gt[0 : layers * cx, 0:cy] + north.T[0 : layers * cx]
    east = (east_in[...] + corner_in[...] * from_south) * from_west
    x_id = lax.broadcasted_iota(jnp.int32, (cx, cy), 0)
    g = [
        grad[k * cx : (k + 1) * cx] + jnp.where(x_id == 0, east[k : k + 1], 0.0)
        for k in range(layers)
    ]
    load.wait()

    def contract(m, c):
        for l in range(levels):
            total = jnp.zeros((cx, cy), F32)
            for t in range(slots):
                total = total + ens_v[m, t, l].astype(F32) * g[t * levels + l]
            con[m * levels + l] = total
            send_w[pl.ds(m * levels + l, 1), :] = total[0:1]
            send_e[pl.ds(m * levels + l, 1), :] = total[cx - 1 : cx]
        return c

    lax.fori_loop(0, members, contract, 0)

    halos = [
        pltpu.make_async_remote_copy(
            src_ref=s, dst_ref=d, send_sem=halo_send.at[i], recv_sem=halo_recv.at[i], device_id=dev,
            device_id_type=MESH)
        for i, (s, d, dev) in enumerate([(send_w, east_h, west_dev), (send_e, west_h, east_dev)])
    ]
    for c in halos:
        c.start()
    for c in halos:
        c.wait()
    to_east = (tx < n_tx - 1).astype(F32)
    to_north = (ty < n_ty - 1).astype(F32)

    def filter_x(i, c):
        mid = con[i]
        before = jnp.where(x_id == 0, west_h[pl.ds(i, 1), :] * from_west, pltpu.roll(mid, 1, 0))
        after = jnp.where(x_id == cx - 1, east_h[pl.ds(i, 1), :] * to_east, pltpu.roll(mid, cx - 1, 0))
        con[i] = 0.25 * before + 0.5 * mid + 0.25 * after
        return c

    planes = members * levels
    lax.fori_loop(0, planes, filter_x, 0)
    e_row = lax.broadcasted_iota(jnp.int32, (8, cy), 0)
    e_lane = lax.broadcasted_iota(jnp.int32, (8, cy), 1)
    pick = jnp.where((e_row == 0) & (e_lane == 0) | (e_row == 1) & (e_lane == cy - 1), 1.0, 0.0)
    edge[...] = dot_nt(pick, con[...].reshape(planes * cx, cy), lax.Precision.HIGHEST)
    up = pltpu.make_async_remote_copy(
        src_ref=edge, dst_ref=edge_s, send_sem=halo_send.at[2], recv_sem=halo_recv.at[2],
        device_id=north_dev, device_id_type=MESH)
    both = [up]
    if n_ty > 2:
        both.append(pltpu.make_async_remote_copy(
            src_ref=edge, dst_ref=edge_n, send_sem=halo_send.at[3], recv_sem=halo_recv.at[3],
            device_id=south_dev, device_id_type=MESH))
    for c in both:
        c.start()
    for c in both:
        c.wait()
    south_row = jnp.where((e_row == 1) & (e_lane == 0), 0.25 * from_south, 0.0)
    north_row = jnp.where((e_row == 0) & (e_lane == cy - 1), 0.25 * to_north, 0.0)

    def outer(e, place):
        return lax.dot_general(e, place, (((0,), (0,)), ((), ())), precision=lax.Precision.HIGHEST,
                               preferred_element_type=F32)

    if n_ty == 2:
        fix = outer(edge_s[...], south_row + north_row)
    else:
        fix = outer(edge_s[...], south_row) + outer(edge_n[...], north_row)
    lane = lax.broadcasted_iota(jnp.int32, (planes * cx, cy), 1)
    mid = con[...].reshape(planes * cx, cy)
    left = jnp.where(lane == 0, 0.0, pltpu.roll(mid, 1, 1))
    right = jnp.where(lane == cy - 1, 0.0, pltpu.roll(mid, cy - 1, 1))
    res = 0.25 * left + 0.5 * mid + 0.25 * right + fix
    out[...] = res.astype(BF16).reshape(out.shape)


def body(mesh_sizes, obs_value, obs_frac, obs_cell, obs_layer, obs_tile, obs_length, ensemble):
    n_tx, n_ty, n_mem = mesh_sizes
    tiles = n_tx * n_ty
    count = obs_value.shape[0]
    hi = pl.cdiv(3 * count // tiles, LO)
    members, slots, levels, cx, cy = ensemble.shape
    layers = slots * levels
    vmem = pl.BlockSpec(memory_space=pltpu.VMEM)
    smem = pl.BlockSpec(memory_space=pltpu.SMEM)
    rows = count // 128
    packed = pl.pallas_call(
        functools.partial(pack_kernel, tiles, hi, cx * cy),
        out_shape=jax.ShapeDtypeStruct((tiles, 4 * hi, LO), F32),
        in_specs=[vmem] * 5 + [smem],
        out_specs=vmem,
        scratch_shapes=[
            pltpu.VMEM((4 * tiles * hi, LO), F32),
            pltpu.VMEM((rows, 128), jnp.int32),
            pltpu.VMEM((rows, 128), jnp.int32),
            pltpu.VMEM((rows, 128), F32),
            pltpu.VMEM((rows, 128), jnp.int32),
        ],
    )(obs_value.reshape(rows, 128), obs_frac, obs_cell.reshape(rows, 128), obs_layer.reshape(rows, 128),
      obs_tile.reshape(rows, 128), obs_length)

    planes = members * levels
    y_rows = up_to(cy + 1, 16)
    square = 2 * cy
    dma = pltpu.SemaphoreType.DMA
    scratch = [
        pltpu.VMEM((tiles, 4 * hi, LO), F32),
        pltpu.VMEM((square, square), F32),
        pltpu.VMEM((y_rows, square), F32),
        pltpu.VMEM((square, square), F32),
        pltpu.VMEM((16, cy), F32),
        pltpu.VMEM((8, square), F32),
        pltpu.VMEM((16, cy), F32),
        pltpu.VMEM((planes, cx, cy), F32),
        pltpu.VMEM((planes, cy), F32),
        pltpu.VMEM((planes, cy), F32),
        pltpu.VMEM((planes, cy), F32),
        pltpu.VMEM((planes, cy), F32),
        pltpu.VMEM((8, planes * cx), F32),
        pltpu.VMEM((8, planes * cx), F32),
        pltpu.VMEM((8, planes * cx), F32),
        pltpu.VMEM(ensemble.shape, BF16),
        dma((tiles,)), dma((tiles,)), dma((2,)), dma((3,)), dma((3,)), dma((4,)), dma((4,)), dma,
    ]
    dims = (n_tx, n_ty, n_mem, hi, layers, cx, cy, members, slots, levels)
    return pl.pallas_call(
        functools.partial(main_kernel, dims),
        out_shape=jax.ShapeDtypeStruct((members, levels, cx, cy), BF16),
        in_specs=[vmem, pl.BlockSpec(memory_space=pl.ANY)],
        out_specs=vmem,
        scratch_shapes=scratch,
        compiler_params=pltpu.CompilerParams(collective_id=0, has_side_effects=True),
    )(packed, ensemble)


def solution(mesh):
    placed = (
        P(("tx", "ty", "mem")),
        P(None, ("tx", "ty", "mem")),
        P(("tx", "ty", "mem")),
        P(("tx", "ty", "mem")),
        P(("tx", "ty", "mem")),
        P(("tx", "ty", "mem")),
        P("mem", None, None, "tx", "ty"),
    )
    sizes = tuple(mesh.shape[a] for a in ("tx", "ty", "mem"))
    return jax.shard_map(
        functools.partial(body, sizes), mesh=mesh, in_specs=placed, out_specs=P("mem", None, "tx", "ty"),
        check_vma=False,
    )
```

time: 211 us -> 54.2 us (0.26)
  matrix products: 84.9 us -> 0 us
  Pallas kernels: 0 us -> 51.6 us
  waiting for transfers between devices: 47.1 us -> 0 us
  starting transfers between devices: 26.9 us -> 0 us
  local copies, waits for them, and re-layouts: 25 us -> 1.72 us
  between operations: 14.4 us -> 0.66 us
  other arithmetic: 11 us -> 0 us
    dot_general x29 -> x0, matrix products: 84.9 us -> none  [the longest x28 83.7 us: contract_rows(): lax.dot_general(left, right, (((0,), (0,)), ((), ())), precision=lax.Prec...]
    pallas_call x0 -> x2, Pallas kernels: none -> 51.6 us  [the longest x1 45.7 us: body(): pl.pallas_call(functools.partial(main_kernel, dims), out_shape=jax.ShapeD...]
    psum x1 -> x0, waiting for transfers between devices: 19.5 us -> none  [body(): grad = lax.psum(interior, 'mem')]
    all_to_all x2 -> x0, waiting for transfers between devices: 17.8 us -> none  [the longest x1 11.2 us: body(): lax.all_to_all(send_floats, ('tx', 'ty'), split_axis=1, concat_axis=1, ti...]
    mul x12 -> x0, local copies, waits for them, and re-layouts: 17.2 us -> none  [spread_rows(): layer_hot[:, :, None] * weight_x[:, None, :]]
    ppermute x6 -> x0, starting transfers between devices: 15 us -> none  [the longest x2 7.05 us: extended_2(): before = lax.ppermute(last, axis, up)]
    all_to_all x2 -> x0, starting transfers between devices: 11.9 us -> none  [the longest x1 8.34 us: body(): lax.all_to_all(send_index, ('tx', 'ty'), split_axis=1, concat_axis=1, til...]
    ppermute x6 -> x0, waiting for transfers between devices: 9.74 us -> none  [the longest x2 8.04 us: extended_2(): after = lax.ppermute(initial, axis, down)]
  transfers between devices with their start and end apart: 9 -> 0, of which waited for: 8 -> 0; matrix products, arithmetic and copies ran while one was open for 2% -> 0% of each run, Pallas kernels for 0% -> 0%
where the time goes in v1:
time: 54.2 us; the launch traced here: 54 us
  Pallas kernels  51.6 us (95%)
  local copies, waits for them, and re-layouts  1.72 us (3%)
  between operations  0.66 us (1%)
    pallas_call x1, Pallas kernels, body(): pl.pallas_call(functools.partial(main_kernel, dims), out_shape=jax.ShapeD...  45.7 us
    pallas_call x1, Pallas kernels, body(): pl.pallas_call(functools.partial(pack_kernel, tiles, hi, cx * cy), out_sh...  5.95 us
    unnamed x1, local copies, waits for them, and re-layouts  1.72 us

profile of v1, /device:TPU:0, one launch (start us, length us, event | category | flops | bytes accessed | tf_op | source)
XLA Modules:
  0.0 54.0 jit_solution(11508118096587162077)
XLA Ops:
  0.7 6.0 %shard_map.73.packed = f32[16,24,256]{2,1,0:T(8,128)} custom-call(f32[64,128]{1,0:T(8,128)} %bitcast.4, f32[2,8192]{1,0:T(2,128)} %frac.1, s32[64,128]{1,0:T(8,128)} %bitcast.5, s32[64,128]{1,0:T(8,128)} %bitcast.6, s32[64,128]{1,0:T(8,128)} %bitcast.7, s32[1]{0:T(128)S(6)} %copy.9.length), custom_call_target="tpu_custom_call" | custom-call | tf_op jit(solution)/shard_map/pallas_call | solution.py:293
  6.6 45.7 %shard_map.74 = bf16[40,2,16,128]{3,2,1,0:T(8,128)(2,1)} custom-call(f32[16,24,256]{2,1,0:T(8,128)} %shard_map.73.packed, bf16[40,6,2,16,128]{4,3,2,1,0:T(8,128)(2,1)} %ens.1), custom_call_target="tpu_custom_call" | custom-call | tf_op jit(solution)/shard_map/pallas_call | solution.py:332
  52.3 1.7 %copy.10 = bf16[40,2,16,128]{3,2,1,0:T(8,128)(2,1)} copy(bf16[40,2,16,128]{3,2,1,0:T(8,128)(2,1)} %shard_map.74) | data formatting | bytes 655360

commit v2 on v1

v2 whole, which is shorter than its diff:
```python
import functools

import jax
import jax.numpy as jnp
from jax import lax
from jax.experimental import pallas as pl
from jax.experimental.pallas import tpu as pltpu
from jax.sharding import PartitionSpec as P

MESH = pl.DeviceIdType.MESH
F32 = jnp.float32
BF16 = jnp.bfloat16
LO = 256


def up_to(n, m):
    return (n + m - 1) // m * m


def split(x):
    high = x.astype(BF16)
    low = (x - high.astype(F32)).astype(BF16)
    return high, low


def dot_nt(a, b, precision=None):
    return lax.dot_general(
        a, b, (((1,), (1,)), ((), ())), precision=precision, preferred_element_type=F32
    )


def flat(rows):
    return jnp.concatenate([rows[i : i + 1] for i in range(rows.shape[0])], axis=1)


def strip(x):
    parts = [
        jnp.broadcast_to(x[i : i + 1], (16, x.shape[1])).astype(BF16) for i in range(x.shape[0])
    ]
    return jnp.concatenate(parts, axis=1)


def tall(x, rows):
    return jnp.concatenate([x] * (rows // 16), axis=0)


def ids(rows, width):
    return lax.broadcasted_iota(jnp.int32, (rows, 128), 0).astype(F32).astype(BF16), width // 128


def wide_ids(rows, width):
    base, times = ids(rows, width)
    return jnp.concatenate([base] * times, axis=1)


def parts_of(x):
    high = x.astype(BF16).astype(F32)
    return strip(high), strip(x - high)


def pick_two(number, first, second, on_first, on_second):
    rows = number.shape[0]
    zero = jnp.zeros((), BF16)
    inner = jnp.where(number == tall(second, rows), tall(on_second, rows), zero)
    return jnp.where(number == tall(first, rows), tall(on_first, rows), inner)


def shift_mix(x, axis, ids_along):
    size = x.shape[axis]
    before = jnp.where(ids_along == 0, 0.0, pltpu.roll(x, 1, axis))
    after = jnp.where(ids_along == size - 1, 0.0, pltpu.roll(x, size - 1, axis))
    return 0.25 * before + 0.5 * x + 0.25 * after


def pack_kernel(tiles, hi, cells, value, frac, cell, layer, tile, length, out, acc, code_s, lo_s, val_s, pos_s):
    rows = value.shape[0]
    lanes = 128
    row_id = lax.broadcasted_iota(jnp.int32, (rows, lanes), 0)
    lane_id = lax.broadcasted_iota(jnp.int32, (rows, lanes), 1)
    tile_v = tile[...]
    masks = [jnp.where(tile_v == t, 1.0, 0.0).astype(F32) for t in range(tiles)]
    stacked = jnp.concatenate(masks, axis=0).astype(BF16)
    a = lax.broadcasted_iota(jnp.int32, (lanes, 2 * lanes), 0)
    b = lax.broadcasted_iota(jnp.int32, (lanes, 2 * lanes), 1)
    upper = jnp.where((a <= b) | (b >= lanes), 1.0, 0.0).astype(BF16)
    sums = jnp.dot(stacked, upper, preferred_element_type=F32)
    totals = jnp.concatenate(
        [sums[t * rows : (t + 1) * rows, lanes:] for t in range(tiles)], axis=1
    ).astype(BF16)
    c = lax.broadcasted_iota(jnp.int32, (rows, rows), 0)
    d = lax.broadcasted_iota(jnp.int32, (rows, rows), 1)
    lower = jnp.where(d < c, 1.0, 0.0).astype(BF16)
    offsets = jnp.dot(lower, totals, preferred_element_type=F32)
    rank = jnp.full((rows, lanes), -1.0, F32)
    for t in range(tiles):
        inner = sums[t * rows : (t + 1) * rows, :lanes] + offsets[:, t * lanes : (t + 1) * lanes]
        rank = rank + masks[t] * inner
    rank = rank.astype(jnp.int32)
    code_s[...] = tile_v * hi + rank // LO
    lo_s[...] = rank % LO
    live = row_id * lanes + lane_id < length[0]
    val_s[...] = jnp.where(live, value[...], 0.0)
    pos_s[...] = layer[...] * cells + cell[...]
    acc[...] = jnp.zeros_like(acc)
    step_rows = 8
    width = step_rows * lanes
    groups = tiles * hi
    group_id = wide_ids(up_to(groups, 16), width)
    lo_id = wide_ids(LO, width)
    one = jnp.ones((), BF16)
    zero = jnp.zeros((), BF16)
    for s in range(rows // step_rows):
        here = pl.ds(s * step_rows, step_rows)
        along = pl.ds(s * width, width)
        code = tall(strip(code_s[here, :].astype(F32)), groups)
        low = tall(strip(lo_s[here, :].astype(F32)), LO)
        low_hot = jnp.where(lo_id == low, one, zero)
        pos = pos_s[here, :]
        pos_low = pos % 128
        fields = [
            parts_of(val_s[here, :]),
            parts_of(frac[0:1, along]),
            parts_of(frac[1:2, along]),
            (strip((pos - pos_low).astype(F32)), strip(pos_low.astype(F32))),
        ]
        mine = group_id == code
        for part in range(2):
            left = jnp.concatenate(
                [jnp.where(mine, tall(f[part], groups), zero) for f in fields], axis=0
            )
            acc[...] += dot_nt(left, low_hot)
    for t in range(tiles):
        for f in range(4):
            start = f * groups + t * hi
            out[t, f * hi : (f + 1) * hi, :] = acc[start : start + hi, :]


def main_kernel(dims, packed, ens, out, recv, acc, acc_in, gt, east_in, north_in, corner_in, con, fix, west_h, east_h,
                send_w, send_e, edge, edge_in, corner_w, corner_e, corner_from_e, corner_from_w, ens_v,
                s_send, s_recv, p_sem, rim_send, rim_recv, halo_send, halo_recv, local_sem):
    n_tx, n_ty, n_mem, hi, layers, cx, cy, members, slots, levels = dims
    tiles = n_tx * n_ty
    tx, ty, mem = lax.axis_index("tx"), lax.axis_index("ty"), lax.axis_index("mem")
    me = tx * n_ty + ty
    load = pltpu.make_async_copy(ens, ens_v, local_sem)
    load.start()
    has_west, has_east = tx > 0, tx < n_tx - 1
    has_south, has_north = ty > 0, ty < n_ty - 1

    barrier = pltpu.get_barrier_semaphore()
    total_devices = tiles * n_mem
    my_id = me * n_mem + mem

    def greet(k, c):
        d = lax.rem(my_id + k, total_devices)
        t = d // n_mem
        pl.semaphore_signal(barrier, inc=1, device_id=(t // n_ty, lax.rem(t, n_ty), lax.rem(d, n_mem)),
                            device_id_type=MESH)
        return c

    lax.fori_loop(1, total_devices, greet, 0)
    partner = (tx, ty, lax.rem(mem + 1, n_mem))
    pl.semaphore_wait(barrier, total_devices - 1)

    def copy_to(t):
        return pltpu.make_async_remote_copy(
            src_ref=packed.at[t], dst_ref=recv.at[me], send_sem=s_send.at[t], recv_sem=s_recv.at[me],
            device_id=(t // n_ty, lax.rem(t, n_ty), mem), device_id_type=MESH)

    def send(k, c):
        copy_to(lax.rem(me + k, tiles)).start()
        return c

    lax.fori_loop(1, tiles, send, 0)

    width = hi * LO
    r_rows = up_to(layers * cx + layers, 16)
    y_rows = up_to(cy + 1, 16)
    r_id = wide_ids(r_rows, width)
    y_id = wide_ids(y_rows, width)
    cells = cx * cy

    def spread(block):
        val, fx, fy, pos = [block[f * hi : (f + 1) * hi] for f in range(4)]
        pos = pos.astype(jnp.int32)
        lay = pos // cells
        col = pos % cells
        x = col // cy
        y = (col % cy).astype(F32)
        c1 = lay * cx + x
        c2 = jnp.where(x == cx - 1, layers * cx + lay, c1 + 1)
        c1, c2 = strip(c1.astype(F32)), strip(c2.astype(F32))
        y1, y2 = strip(y), strip(y + 1.0)
        near, far = parts_of(val * (1.0 - fx)), parts_of(val * fx)
        low, high = parts_of(1.0 - fy), parts_of(fy)
        lh, ll = [pick_two(r_id, c1, c2, near[i], far[i]) for i in range(2)]
        rh, rl = [pick_two(y_id, y1, y2, low[i], high[i]) for i in range(2)]
        acc[0:y_rows, 0:r_rows] += dot_nt(rh, lh) + dot_nt(rl, lh) + dot_nt(rh, ll)

    acc[...] = jnp.zeros_like(acc)

    @pl.when(jnp.logical_not(has_west))
    def _():
        east_in[...] = jnp.zeros_like(east_in)
        west_h[...] = jnp.zeros_like(west_h)

    @pl.when(jnp.logical_not(has_east))
    def _():
        east_h[...] = jnp.zeros_like(east_h)

    @pl.when(jnp.logical_not(has_south))
    def _():
        north_in[...] = jnp.zeros_like(north_in)

    @pl.when(jnp.logical_not(has_south & has_west))
    def _():
        corner_in[...] = jnp.zeros_like(corner_in)

    spread(packed[me])

    def receive(k, c):
        src = lax.rem(me + tiles - k, tiles)
        pltpu.make_async_remote_copy(
            src_ref=packed.at[src], dst_ref=recv.at[src], send_sem=s_send.at[src], recv_sem=s_recv.at[src],
            device_id=partner, device_id_type=MESH).wait_recv()
        spread(recv[src])
        return c

    lax.fori_loop(1, tiles, receive, 0)

    swap = pltpu.make_async_remote_copy(
        src_ref=acc.at[pl.ds(0, y_rows)], dst_ref=acc_in, send_sem=p_sem.at[0], recv_sem=p_sem.at[1],
        device_id=partner, device_id_type=MESH)
    swap.start()

    def remote(src, dst, send_sem, recv_sem, dev):
        return pltpu.make_async_remote_copy(src_ref=src, dst_ref=dst, send_sem=send_sem, recv_sem=recv_sem,
                                            device_id=dev, device_id_type=MESH)

    def start(copies):
        for c, sends, _ in copies:
            pl.when(sends)(c.start)

    def finish(copies):
        for c, sends, gets in copies:
            pl.when(gets)(c.wait_recv)
            pl.when(sends)(c.wait_send)

    e_tx, w_tx = lax.rem(tx + 1, n_tx), lax.rem(tx + n_tx - 1, n_tx)
    n_ty_id, s_ty_id = lax.rem(ty + 1, n_ty), lax.rem(ty + n_ty - 1, n_ty)
    rim_rows = pl.ds(layers * cx, 16)
    rims = []
    for q in range(n_mem):
        other = lax.rem(mem + q, n_mem)
        rims.append((remote(acc.at[pl.ds(cy, 8)], north_in.at[q], rim_send.at[0, q], rim_recv.at[0, q],
                            (tx, n_ty_id, other)), has_north, has_south))
    start(rims)
    gt[...] = acc[...].T
    late = []
    for q in range(n_mem):
        other = lax.rem(mem + q, n_mem)
        late.append((remote(gt.at[rim_rows, pl.ds(0, cy)], east_in.at[q], rim_send.at[1, q], rim_recv.at[1, q],
                            (e_tx, ty, other)), has_east, has_west))
        late.append((remote(gt.at[rim_rows, pl.ds(cy, cy)], corner_in.at[q], rim_send.at[2, q], rim_recv.at[2, q],
                            (e_tx, n_ty_id, other)), has_east & has_north, has_west & has_south))
    start(late)

    def drain(k, c):
        copy_to(lax.rem(me + k, tiles)).wait_send()
        return c

    lax.fori_loop(1, tiles, drain, 0)
    swap.wait()
    joined = jnp.concatenate([acc_in[...], jnp.zeros((2 * cy - y_rows, acc_in.shape[1]), F32)], axis=0).T
    grad = gt[0 : layers * cx, 0:cy] + joined[0 : layers * cx, 0:cy]
    finish(rims + late)
    north = sum(north_in[q] for q in range(n_mem))
    north = jnp.concatenate([north, jnp.zeros((cy - 8, north.shape[1]), F32)], axis=0)
    grad = grad + north.T[0 : layers * cx]
    east = sum(east_in[q] + corner_in[q] for q in range(n_mem))
    x_id = lax.broadcasted_iota(jnp.int32, (cx, cy), 0)
    g = [
        grad[k * cx : (k + 1) * cx] + jnp.where(x_id == 0, east[k : k + 1], 0.0)
        for k in range(layers)
    ]
    load.wait()

    def contract(m, c):
        for l in range(levels):
            total = jnp.zeros((cx, cy), F32)
            for t in range(slots):
                total = total + ens_v[m, t, l].astype(F32) * g[t * levels + l]
            con[m * levels + l] = total
            send_w[pl.ds(m * levels + l, 1), :] = total[0:1]
            send_e[pl.ds(m * levels + l, 1), :] = total[cx - 1 : cx]
        return c

    lax.fori_loop(0, members, contract, 0, unroll=2)

    def halo(i, src, dst, dev, sends, gets):
        return (remote(src, dst, halo_send.at[i], halo_recv.at[i], dev), sends, gets)

    sides = [halo(0, send_w, east_h, (w_tx, ty, mem), has_west, has_east),
             halo(1, send_e, west_h, (e_tx, ty, mem), has_east, has_west)]
    start(sides)
    planes = members * levels
    e_row = lax.broadcasted_iota(jnp.int32, (8, cy), 0)
    e_lane = lax.broadcasted_iota(jnp.int32, (8, cy), 1)
    pick = jnp.where((e_row == 0) & (e_lane == 0) | (e_row == 1) & (e_lane == cy - 1), 1.0, 0.0)
    exact = lax.Precision.HIGHEST
    corner_w[...] = dot_nt(pick, send_w[...], exact)
    corner_e[...] = dot_nt(pick, send_e[...], exact)
    edge[...] = dot_nt(pick, con[...].reshape(planes * cx, cy), exact)
    south = jnp.where((e_row == 1) & (e_lane == 0) & has_south, 0.25, 0.0)
    north = jnp.where((e_row == 0) & (e_lane == cy - 1) & has_north, 0.25, 0.0)
    always = tx >= 0
    places = [south + north] if n_ty == 2 else [south, north]
    targets = [n_ty_id, s_ty_id][: len(places)]
    for i, t in enumerate(targets):
        sides += [
            halo(2 + 3 * i, edge, edge_in.at[i], (tx, t, mem), always, always),
            halo(3 + 3 * i, corner_w, corner_from_e.at[i], (w_tx, t, mem), has_west, has_east),
            halo(4 + 3 * i, corner_e, corner_from_w.at[i], (e_tx, t, mem), has_east, has_west),
        ]
        pl.when(jnp.logical_not(has_east))(functools.partial(fill, corner_from_e, i))
        pl.when(jnp.logical_not(has_west))(functools.partial(fill, corner_from_w, i))
    start(sides[2:])

    batch = max(b for b in range(1, 11) if planes % b == 0)
    lane = lax.broadcasted_iota(jnp.int32, (batch * cx, cy), 1)
    x_in = lax.broadcasted_iota(jnp.int32, (batch * cx, cy), 0) % cx

    def local(i, c):
        here = pl.ds(i * batch, batch)
        mid = shift_mix(con[here].reshape(batch * cx, cy), 1, lane)
        before = jnp.where(x_in == 0, 0.0, pltpu.roll(mid, 1, 0))
        after = jnp.where(x_in == cx - 1, 0.0, pltpu.roll(mid, batch * cx - 1, 0))
        con[here] = (0.25 * before + 0.5 * mid + 0.25 * after).reshape(batch, cx, cy)
        return c

    lax.fori_loop(0, planes // batch, local, 0)
    finish(sides)

    def outer(e, place):
        return lax.dot_general(e, place, (((0,), (0,)), ((), ())), precision=exact, preferred_element_type=F32)

    l_in = lax.broadcasted_iota(jnp.int32, (8, planes * cx), 1) % cx
    row_lane = lax.broadcasted_iota(jnp.int32, (planes, cy), 1)
    west = shift_mix(west_h[...], 1, row_lane)
    east = shift_mix(east_h[...], 1, row_lane)
    added = jnp.zeros((planes * cx, cy), F32)
    for i, place in enumerate(places):
        e = edge_in[i]
        before = jnp.where(l_in == 0, 0.0, pltpu.roll(e, 1, 1))
        after = jnp.where(l_in == cx - 1, 0.0, pltpu.roll(e, planes * cx - 1, 1))
        added = added + outer(0.25 * before + 0.5 * e + 0.25 * after, place)
        west = west + outer(corner_from_w[i], place)
        east = east + outer(corner_from_e[i], place)
    fix[...] = added.reshape(planes, cx, cy)
    west_h[...] = 0.25 * west
    east_h[...] = 0.25 * east

    def last(m, c):
        for l in range(levels):
            i = m * levels + l
            res = con[i] + fix[i]
            res = res + jnp.where(x_id == 0, west_h[pl.ds(i, 1), :], 0.0)
            res = res + jnp.where(x_id == cx - 1, east_h[pl.ds(i, 1), :], 0.0)
            out[m, l] = res.astype(BF16)
        return c

    lax.fori_loop(0, members, last, 0, unroll=2)


def fill(ref, i):
    ref[i] = jnp.zeros(ref.shape[1:], F32)


def body(mesh_sizes, obs_value, obs_frac, obs_cell, obs_layer, obs_tile, obs_length, ensemble):
    n_tx, n_ty, n_mem = mesh_sizes
    tiles = n_tx * n_ty
    count = obs_value.shape[0]
    hi = pl.cdiv(3 * count // tiles, LO)
    members, slots, levels, cx, cy = ensemble.shape
    layers = slots * levels
    vmem = pl.BlockSpec(memory_space=pltpu.VMEM)
    smem = pl.BlockSpec(memory_space=pltpu.SMEM)
    rows = count // 128
    packed = pl.pallas_call(
        functools.partial(pack_kernel, tiles, hi, cx * cy),
        out_shape=jax.ShapeDtypeStruct((tiles, 4 * hi, LO), F32),
        in_specs=[vmem] * 5 + [smem],
        out_specs=vmem,
        scratch_shapes=[
            pltpu.VMEM((4 * tiles * hi, LO), F32),
            pltpu.VMEM((rows, 128), jnp.int32),
            pltpu.VMEM((rows, 128), jnp.int32),
            pltpu.VMEM((rows, 128), F32),
            pltpu.VMEM((rows, 128), jnp.int32),
        ],
    )(obs_value.reshape(rows, 128), obs_frac, obs_cell.reshape(rows, 128), obs_layer.reshape(rows, 128),
      obs_tile.reshape(rows, 128), obs_length)

    planes = members * levels
    y_rows = up_to(cy + 1, 16)
    square = 2 * cy
    sides = 1 if n_ty == 2 else 2
    dma = pltpu.SemaphoreType.DMA
    scratch = [
        pltpu.VMEM((tiles, 4 * hi, LO), F32),
        pltpu.VMEM((square, square), F32),
        pltpu.VMEM((y_rows, square), F32),
        pltpu.VMEM((square, square), F32),
        pltpu.VMEM((n_mem, 16, cy), F32),
        pltpu.VMEM((n_mem, 8, square), F32),
        pltpu.VMEM((n_mem, 16, cy), F32),
        pltpu.VMEM((planes, cx, cy), F32),
        pltpu.VMEM((planes, cx, cy), F32),
        pltpu.VMEM((planes, cy), F32),
        pltpu.VMEM((planes, cy), F32),
        pltpu.VMEM((planes, cy), F32),
        pltpu.VMEM((planes, cy), F32),
        pltpu.VMEM((8, planes * cx), F32),
        pltpu.VMEM((sides, 8, planes * cx), F32),
        pltpu.VMEM((8, planes), F32),
        pltpu.VMEM((8, planes), F32),
        pltpu.VMEM((sides, 8, planes), F32),
        pltpu.VMEM((sides, 8, planes), F32),
        pltpu.VMEM(ensemble.shape, BF16),
        dma((tiles,)), dma((tiles,)), dma((2,)), dma((3, n_mem)), dma((3, n_mem)),
        dma((2 + 3 * sides,)), dma((2 + 3 * sides,)), dma,
    ]
    dims = (n_tx, n_ty, n_mem, hi, layers, cx, cy, members, slots, levels)
    return pl.pallas_call(
        functools.partial(main_kernel, dims),
        out_shape=jax.ShapeDtypeStruct((members, levels, cx, cy), BF16),
        in_specs=[vmem, pl.BlockSpec(memory_space=pl.ANY)],
        out_specs=vmem,
        scratch_shapes=scratch,
        compiler_params=pltpu.CompilerParams(collective_id=0, has_side_effects=True),
    )(packed, ensemble)


def solution(mesh):
    placed = (
        P(("tx", "ty", "mem")),
        P(None, ("tx", "ty", "mem")),
        P(("tx", "ty", "mem")),
        P(("tx", "ty", "mem")),
        P(("tx", "ty", "mem")),
        P(("tx", "ty", "mem")),
        P("mem", None, None, "tx", "ty"),
    )
    sizes = tuple(mesh.shape[a] for a in ("tx", "ty", "mem"))
    return jax.shard_map(
        functools.partial(body, sizes), mesh=mesh, in_specs=placed, out_specs=P("mem", None, "tx", "ty"),
        check_vma=False,
    )
```

time: 54.2 us -> 42.8 us (0.79)
  Pallas kernels: 51.6 us -> 40.2 us
    pallas_call x1, Pallas kernels: 45.7 us -> 34.5 us  [body(): pl.pallas_call(functools.partial(main_kernel, dims), out_shape=jax.ShapeD...]
where the time goes in v2:
time: 42.8 us; the launch traced here: 42.6 us
  Pallas kernels  40.2 us (94%)
  local copies, waits for them, and re-layouts  1.72 us (4%)
  between operations  0.66 us (2%)
    pallas_call x1, Pallas kernels, body(): pl.pallas_call(functools.partial(main_kernel, dims), out_shape=jax.ShapeD...  34.5 us
    pallas_call x1, Pallas kernels, body(): pl.pallas_call(functools.partial(pack_kernel, tiles, hi, cx * cy), out_sh...  5.68 us
    unnamed x1, local copies, waits for them, and re-layouts  1.72 us

profile of v2, /device:TPU:0, one launch (start us, length us, event | category | flops | bytes accessed | tf_op | source)
XLA Modules:
  0.0 42.6 jit_solution(207549750694677142)
XLA Ops:
  0.7 5.7 %shard_map.73.packed = f32[16,24,256]{2,1,0:T(8,128)} custom-call(f32[64,128]{1,0:T(8,128)} %bitcast.4, f32[2,8192]{1,0:T(2,128)} %frac.1, s32[64,128]{1,0:T(8,128)} %bitcast.5, s32[64,128]{1,0:T(8,128)} %bitcast.6, s32[64,128]{1,0:T(8,128)} %bitcast.7, s32[1]{0:T(128)S(6)} %copy.9.length), custom_call_target="tpu_custom_call" | custom-call | tf_op jit(solution)/shard_map/pallas_call | solution.py:389
  6.3 34.5 %shard_map.74 = bf16[40,2,16,128]{3,2,1,0:T(8,128)(2,1)} custom-call(f32[16,24,256]{2,1,0:T(8,128)} %shard_map.73.packed, bf16[40,6,2,16,128]{4,3,2,1,0:T(8,128)(2,1)} %ens.1), custom_call_target="tpu_custom_call" | custom-call | tf_op jit(solution)/shard_map/pallas_call | solution.py:434
  40.9 1.7 %copy.10 = bf16[40,2,16,128]{3,2,1,0:T(8,128)(2,1)} copy(bf16[40,2,16,128]{3,2,1,0:T(8,128)(2,1)} %shard_map.74) | data formatting | bytes 655360

commit v3 on v2

--- a/solution.py
+++ b/solution.py
@@ -124,11 +124,11 @@
             (strip((pos - pos_low).astype(F32)), strip(pos_low.astype(F32))),
         ]
         mine = group_id == code
-        for part in range(2):
-            left = jnp.concatenate(
-                [jnp.where(mine, tall(f[part], groups), zero) for f in fields], axis=0
-            )
-            acc[...] += dot_nt(left, low_hot)
+        left = jnp.concatenate(
+            [jnp.where(mine, tall(f[part], groups), zero) for part in range(2) for f in fields], axis=0
+        )
+        both = dot_nt(left, low_hot)
+        acc[...] += both[: 4 * groups] + both[4 * groups :]
     for t in range(tiles):
         for f in range(4):
             start = f * groups + t * hi
@@ -195,7 +195,8 @@
         low, high = parts_of(1.0 - fy), parts_of(fy)
         lh, ll = [pick_two(r_id, c1, c2, near[i], far[i]) for i in range(2)]
         rh, rl = [pick_two(y_id, y1, y2, low[i], high[i]) for i in range(2)]
-        acc[0:y_rows, 0:r_rows] += dot_nt(rh, lh) + dot_nt(rl, lh) + dot_nt(rh, ll)
+        both = dot_nt(jnp.concatenate([rh, rl], axis=0), lh)
+        acc[0:y_rows, 0:r_rows] += both[:y_rows] + both[y_rows:] + dot_nt(rh, ll)
 
     acc[...] = jnp.zeros_like(acc)
 

time: 42.8 us -> 40.3 us (0.942)
  Pallas kernels: 40.2 us -> 37.6 us
    pallas_call x1, Pallas kernels: 34.5 us -> 31.9 us  [body(): pl.pallas_call(functools.partial(main_kernel, dims), out_shape=jax.ShapeD...]
where the time goes in v3:
time: 40.3 us; the launch traced here: 40 us
  Pallas kernels  37.6 us (93%)
  local copies, waits for them, and re-layouts  1.72 us (4%)
  between operations  0.66 us (2%)
    pallas_call x1, Pallas kernels, body(): pl.pallas_call(functools.partial(main_kernel, dims), out_shape=jax.ShapeD...  31.9 us
    pallas_call x1, Pallas kernels, body(): pl.pallas_call(functools.partial(pack_kernel, tiles, hi, cx * cy), out_sh...  5.7 us
    unnamed x1, local copies, waits for them, and re-layouts  1.72 us

profile of v3, /device:TPU:0, one launch (start us, length us, event | category | flops | bytes accessed | tf_op | source)
XLA Modules:
  0.0 40.0 jit_solution(15081211975052576382)
XLA Ops:
  0.7 5.7 %shard_map.73.packed = f32[16,24,256]{2,1,0:T(8,128)} custom-call(f32[64,128]{1,0:T(8,128)} %bitcast.4, f32[2,8192]{1,0:T(2,128)} %frac.1, s32[64,128]{1,0:T(8,128)} %bitcast.5, s32[64,128]{1,0:T(8,128)} %bitcast.6, s32[64,128]{1,0:T(8,128)} %bitcast.7, s32[1]{0:T(128)S(6)} %copy.9.length), custom_call_target="tpu_custom_call" | custom-call | tf_op jit(solution)/shard_map/pallas_call | solution.py:390
  6.4 31.9 %shard_map.74 = bf16[40,2,16,128]{3,2,1,0:T(8,128)(2,1)} custom-call(f32[16,24,256]{2,1,0:T(8,128)} %shard_map.73.packed, bf16[40,6,2,16,128]{4,3,2,1,0:T(8,128)(2,1)} %ens.1), custom_call_target="tpu_custom_call" | custom-call | tf_op jit(solution)/shard_map/pallas_call | solution.py:435
  38.3 1.7 %copy.10 = bf16[40,2,16,128]{3,2,1,0:T(8,128)(2,1)} copy(bf16[40,2,16,128]{3,2,1,0:T(8,128)(2,1)} %shard_map.74) | data formatting | bytes 655360
